TPU v7x, 128 devices: a whole 4x4x4 slice. The times are simulated.
128 devices in a mesh: rep: 1, dp: 128 (over x, y, z, core).
Axes of the slice: x: 4, y: 4, z: 4, core: 2. Of those that a mesh axis runs over, the one named last changes fastest.
Arguments:
- g_w_gate: bfloat16 [128, 2, 896, 2560], P(('rep', 'dp'))
- g_w_up: bfloat16 [128, 2, 896, 2560], P(('rep', 'dp'))
- g_w_down: bfloat16 [128, 2, 2560, 896], P(('rep', 'dp'))
- w_gate: bfloat16 [2, 896, 2560], replicated
- w_up: bfloat16 [2, 896, 2560], replicated
- w_down: bfloat16 [2, 2560, 896], replicated
- m_w_gate: float32 [2, 896, 2560], P(None, 'dp')
- m_w_up: float32 [2, 896, 2560], P(None, 'dp')
- m_w_down: float32 [2, 2560, 896], P(None, 'dp')
- v_w_gate: float32 [2, 896, 2560], P(None, 'dp')
- v_w_up: float32 [2, 896, 2560], P(None, 'dp')
- v_w_down: float32 [2, 2560, 896], P(None, 'dp')
Outputs:
- output 1: bfloat16 [2, 896, 2560], P('rep')
- output 2: bfloat16 [2, 896, 2560], P('rep')
- output 3: bfloat16 [2, 2560, 896], P('rep')
- output 4: float32 [2, 896, 2560], P('rep', 'dp')
- output 5: float32 [2, 896, 2560], P('rep', 'dp')
- output 6: float32 [2, 2560, 896], P('rep', 'dp')
- output 7: float32 [2, 896, 2560], P('rep', 'dp')
- output 8: float32 [2, 896, 2560], P('rep', 'dp')
- output 9: float32 [2, 2560, 896], P('rep', 'dp')
All inputs are finite; a program needn't handle non-finite values.
Results may differ from a plain program's by a relative error of at most 0.022.
Values are sent between devices in bfloat16 or wider.
A program may use at most 1.5 GiB of HBM per device.

v0:
```python
import jax
import jax.numpy as jnp
from jax import lax
from jax.sharding import PartitionSpec as P


def adamw(w, m, v, g):
    m = 0.9 * m + 0.1 * g
    v = 0.95 * v + 0.05 * g * g
    step = m * lax.rsqrt(v + 1e-8) + 0.1 * w
    return (w - 0.02 * step).astype(jnp.bfloat16), m, v


def clipped(gradients, sum_of_squares, count):
    factor = jnp.minimum(1.0, 0.5 * lax.rsqrt(sum_of_squares / count + 1e-30))
    return [g * factor for g in gradients]


def solution(mesh):
    def step(*arrays):
        terms, weights, m, v = (arrays[i : i + 3] for i in (0, 3, 6, 9))
        gradients = [lax.psum_scatter(t[0], "dp", scatter_dimension=1, tiled=True).astype(jnp.float32) for t in terms]
        squares = lax.psum(sum(jnp.sum(g * g) for g in gradients), "dp")
        gradients = clipped(gradients, squares, lax.psum(1, "dp") * sum(g.size for g in gradients))
        me = lax.axis_index("dp")
        own = [lax.dynamic_slice_in_dim(w, me * one.shape[1], one.shape[1], 1).astype(jnp.float32) for w, one in zip(weights, m, strict=True)]
        new = [adamw(w, m, v, g) for w, m, v, g in zip(own, m, v, gradients, strict=True)]
        whole = [lax.all_gather(one[0], "dp", axis=1, tiled=True) for one in new]
        return (*whole, *(one[1] for one in new), *(one[2] for one in new))

    all_of, cut = P(None, None, None), P(None, "dp", None)
    return jax.shard_map(
        step,
        mesh=mesh,
        in_specs=(P(("rep", "dp"), None, None, None),) * 3 + (all_of,) * 3 + (cut,) * 6,
        out_specs=(P("rep", None, None),) * 3 + (P("rep", "dp", None),) * 6,
        check_vma=False,
    )
```

profile of v0, /device:TPU:1, one launch (start us, length us, event | category | flops | bytes accessed | tf_op | source)
XLA Modules:
  0.0 634.2 jit_solution(8133891588135615865)
XLA Ops:
  7.2 0.0 all-reduce.6.cloned.1.call-start
  7.2 0.0 copy-start
  7.2 0.0 slice-start
  7.2 0.0 slice-start.1
  7.3 41.0 %copy.48 = bf16[1,2,2560,896]{3,1,2,0:T(2,128)(2,1)} copy(bf16[1,2,2560,896]{3,2,1,0:T(8,128)(2,1)} %param.14) | data formatting | bytes 18350080 | tf_op args[2]
  48.2 0.0 copy-done
  48.2 0.0 slice-start.2
  48.2 26.1 %copy.49 = bf16[1,2,896,2560]{3,1,2,0:T(2,128)(2,1)} copy(bf16[1,2,896,2560]{3,2,1,0:T(8,128)(2,1)S(1)} %copy-done) | data formatting | bytes 18350080 | tf_op args[1]
  74.4 0.0 slice-done
  74.4 0.0 slice-done.1
  74.4 0.0 slice-done.2
  74.4 26.1 %copy.50 = bf16[1,2,896,2560]{3,1,2,0:T(2,128)(2,1)} copy(bf16[1,2,896,2560]{3,2,1,0:T(8,128)(2,1)S(1)} %bitcast.13) | data formatting | bytes 18350080 | tf_op args[0]
  100.5 0.0 copy-start.1
  100.5 0.0 copy-start.2
  100.5 0.0 copy-start.3
  100.5 0.0 copy-start.4
  100.5 0.0 copy-start.5
  100.5 0.0 copy-start.6
  100.6 0.0 all-reduce.6.cloned.1.call-update
  100.6 0.0 all-gather.6.cloned.1.call-start
  100.6 236.0 %all-reduce.6.cloned.1.call-done = (bf16[2,896,2560]{2,0,1:T(2,128)(2,1)}, bf16[2,896,2560]{2,0,1:T(2,128)(2,1)}, bf16[2,2560,896]{2,0,1:T(2,128)(2,1)}) async-done(((bf16[2,896,2560]{2,0,1:T(2,128)(2,1)}, bf16[2,896,2560]{2,0,1:T(2,128)(2,1)}, bf16[2,2560,896]{2,0,1:T(2,128)(2,1)}), (bf16[2,896,2560]{2,0,1:T(2,128)(2,1)}, bf16[2,896,2560]{2,0,1:T(2,128)(2,1)}, ...) | async-done | bytes 27525136
  336.6 1.7 fusion.8
  339.6 1.6 fusion.10
  341.9 1.1 constant_dynamic-slice_fusion.1
  342.9 64.9 %psum.7 = f32[]{:T(128)} all-reduce(f32[]{:T(128)S(6)} %add.65), channel_id=1, replica_groups=mesh['rep'=1,'dp'=128] {'dp'}, use_global_device_ids=true, to_apply=%region_6.0 | all-reduce | flops 1 | bytes 8 | tf_op jit(solution)/shard_map/psum | solution.py:23
  408.5 0.0 copy-done.1
  408.5 0.0 copy-done.2
  408.5 2.0 fusion.19
  410.5 0.0 all-gather.6.cloned.1.call-update
  410.5 0.0 all-gather.4.cloned.1.call-start
  410.6 0.0 copy-done.3
  410.6 0.0 copy-done.4
  410.6 2.0 fusion.18
  412.6 0.0 all-gather.4.cloned.1.call-update
  412.6 0.2 all-gather.8.cloned.1.call-start
  412.8 0.9 constant_dynamic-slice_fusion
  413.8 0.0 copy-done.5
  413.8 0.0 copy-done.6
  413.8 2.0 fusion.20
  415.8 0.0 all-gather.8.cloned.1.call-update
  415.8 61.2 %all-gather.6.cloned.1.call-done = bf16[2,896,2560]{2,0,1:T(2,128)(2,1)} async-done(((bf16[2,7,2560]{2,0,1:T(2,128)(2,1)}), bf16[2,896,2560]{2,0,1:T(2,128)(2,1)}) %all-gather.6.cloned.1.call-update) | async-done | bytes 9175056 | tf_op jit(solution)/shard_map/all_gather | solution.py:28
  477.0 8.7 %copy.37 = bf16[2,896,2560]{2,1,0:T(8,128)(2,1)} copy(bf16[2,896,2560]{2,0,1:T(2,128)(2,1)} %all-gather.6.cloned.1.call-done) | data formatting | bytes 18350080
  485.7 62.8 %all-gather.4.cloned.1.call-done = bf16[2,896,2560]{2,0,1:T(2,128)(2,1)} async-done(((bf16[2,7,2560]{2,0,1:T(2,128)(2,1)}), bf16[2,896,2560]{2,0,1:T(2,128)(2,1)}) %all-gather.4.cloned.1.call-update) | async-done | bytes 9175056 | tf_op jit(solution)/shard_map/all_gather | solution.py:28
  548.5 8.7 %copy.36 = bf16[2,896,2560]{2,1,0:T(8,128)(2,1)} copy(bf16[2,896,2560]{2,0,1:T(2,128)(2,1)} %all-gather.4.cloned.1.call-done) | data formatting | bytes 18350080
  557.2 62.0 %all-gather.8.cloned.1.call-done = bf16[2,2560,896]{2,0,1:T(2,128)(2,1)} async-done(((bf16[2,20,896]{2,0,1:T(2,128)(2,1)}), bf16[2,2560,896]{2,0,1:T(2,128)(2,1)}) %all-gather.8.cloned.1.call-update) | async-done | bytes 9175056 | tf_op jit(solution)/shard_map/all_gather | solution.py:28
  619.2 8.4 %copy.38 = bf16[2,2560,896]{2,1,0:T(8,128)(2,1)} copy(bf16[2,2560,896]{2,0,1:T(2,128)(2,1)} %all-gather.8.cloned.1.call-done) | data formatting | bytes 18350080
  (1 shorter events, 0.0 us)
Async XLA Ops:
  7.2 329.4 %all-reduce.6.cloned.1.call-start = ((), (), s32[]{:S(2)}) async-start(), calls=%async_computation.3 | async-start | bytes 55050240
  7.2 41.0 %copy-start = (bf16[1,2,896,2560]{3,2,1,0:T(8,128)(2,1)S(1)}, bf16[1,2,896,2560]{3,2,1,0:T(8,128)(2,1)}, u32[]{:S(2)}) copy-start(bf16[1,2,896,2560]{3,2,1,0:T(8,128)(2,1)} %param.13) | copy-start | bytes 27525124
  7.2 67.1 %slice-start = ((s8[9175040]{0:T(1024)(128)(4,1)}), s8[4194304]{0:T(1024)(128)(4,1)S(1)}, s32[]{:S(2)}) async-start(s8[9175040]{0:T(1024)(128)(4,1)} %bitcast.12), calls=%async_computation.4 | async-start | bytes 8388608
  7.2 67.1 %slice-start.1 = ((s8[9175040]{0:T(1024)(128)(4,1)}), s8[4194304]{0:T(1024)(128)(4,1)S(1)}, s32[]{:S(2)}) async-start(s8[9175040]{0:T(1024)(128)(4,1)} %bitcast.12), calls=%async_computation.5 | async-start | bytes 8388608
  48.2 26.1 %slice-start.2 = ((s8[9175040]{0:T(1024)(128)(4,1)}), s8[786432]{0:T(1024)(128)(4,1)S(1)}, s32[]{:S(2)}) async-start(s8[9175040]{0:T(1024)(128)(4,1)} %bitcast.12), calls=%async_computation.6 | async-start | bytes 1572864
  100.5 308.0 %copy-start.1 = (f32[2,7,2560]{2,0,1:T(2,128)S(1)}, f32[2,7,2560]{2,0,1:T(2,128)}, u32[]{:S(2)}) copy-start(f32[2,7,2560]{2,0,1:T(2,128)} %param.22) | copy-start | bytes 430084
  100.5 308.0 %copy-start.2 = (f32[2,7,2560]{2,0,1:T(2,128)S(1)}, f32[2,7,2560]{2,0,1:T(2,128)}, u32[]{:S(2)}) copy-start(f32[2,7,2560]{2,0,1:T(2,128)} %param.19) | copy-start | bytes 430084
  100.5 310.1 %copy-start.3 = (f32[2,7,2560]{2,0,1:T(2,128)S(1)}, f32[2,7,2560]{2,0,1:T(2,128)}, u32[]{:S(2)}) copy-start(f32[2,7,2560]{2,0,1:T(2,128)} %param.21) | copy-start | bytes 430084
  100.5 310.1 %copy-start.4 = (f32[2,7,2560]{2,0,1:T(2,128)S(1)}, f32[2,7,2560]{2,0,1:T(2,128)}, u32[]{:S(2)}) copy-start(f32[2,7,2560]{2,0,1:T(2,128)} %param.18) | copy-start | bytes 430084
  100.5 313.2 %copy-start.5 = (f32[2,20,896]{2,0,1:T(2,128)S(1)}, f32[2,20,896]{2,0,1:T(2,128)}, u32[]{:S(2)}) copy-start(f32[2,20,896]{2,0,1:T(2,128)} %param.23) | copy-start | bytes 430084
  100.5 313.2 %copy-start.6 = (f32[2,20,896]{2,0,1:T(2,128)S(1)}, f32[2,20,896]{2,0,1:T(2,128)}, u32[]{:S(2)}) copy-start(f32[2,20,896]{2,0,1:T(2,128)} %param.20) | copy-start | bytes 430084
  100.6 376.5 %all-gather.6.cloned.1.call-start = ((), (), s32[]{:S(2)}) async-start(), calls=%async_computation.1 | async-start | bytes 9246720 | tf_op jit(solution)/shard_map/all_gather | solution.py:28
  410.5 138.0 %all-gather.4.cloned.1.call-start = ((), (), s32[]{:S(2)}) async-start(), calls=%async_computation | async-start | bytes 9246720 | tf_op jit(solution)/shard_map/all_gather | solution.py:28
  412.6 206.6 %all-gather.8.cloned.1.call-start = ((), (), s32[]{:S(2)}) async-start(), calls=%async_computation.2 | async-start | bytes 9246720 | tf_op jit(solution)/shard_map/all_gather | solution.py:28
Sparse Core Ops, SparseCore 0:
  100.7 235.8 all-reduce.5
  410.6 66.3 all-gather.5
  480.6 67.7 all-gather.3
  551.4 67.7 all-gather.7
where the time goes:
time: 635 us; the launch traced here: 634 us
  waiting for transfers between devices  422 us (66%)
  local copies, waits for them, and re-layouts  121 us (19%)
  blocking collectives  64.9 us (10%)
  between operations  16.6 us (3%)
  other arithmetic  9.24 us (1%)
    unnamed x5, waiting for transfers between devices  236 us
    all_gather x3, waiting for transfers between devices, step(): whole = [lax.all_gather(one[0], 'dp', axis=1, tiled=True) for one in new]  186 us
    unnamed x26, local copies, waits for them, and re-layouts  119 us
    psum x1, blocking collectives, step(): squares = lax.psum(sum((jnp.sum(g * g) for g in gradients)), 'dp')  64.9 us
  transfers between devices with their start and end apart: 4, of which 4 were waited for; matrix products, arithmetic and copies ran while one was open for 4% of the time, Pallas kernels for 0%

commit v1 on v0

v1 whole, which is shorter than its diff:
```python
import functools

import jax
import jax.numpy as jnp
from jax import lax
from jax.experimental import pallas as pl
from jax.experimental.pallas import tpu as pltpu
from jax.sharding import PartitionSpec as P

MESH = pl.DeviceIdType.MESH
F32, BF16 = jnp.float32, jnp.bfloat16
X, Y, Z = 0, 1, 2
RIGHT, LEFT = 0, 1
PLAIN, DOWN = (0, 1), (2, 3)
GROUP, OTHERS, STEPS = range(8), range(1, 8), (1, 2, 3)
VMEM_LIMIT = 60 * 2**20


def div(a, n):
    return lax.div(a, jnp.int32(n))


def rem(a, n):
    return lax.rem(a, jnp.int32(n))


class Place:
    def __init__(self):
        i = lax.axis_index("dp")
        self.c = rem(i, 2)
        self.at = (div(i, 32), rem(div(i, 8), 4), rem(div(i, 2), 4))
        self.j = rem(i, 8)

    def device(self, at, c):
        return {"dp": ((at[0] * 4 + at[1]) * 4 + at[2]) * 2 + c}

    def along(self, axis, by):
        to = rem(self.at[axis] + (by + 4), 4)
        at = tuple(to if a == axis else v for a, v in enumerate(self.at))
        return self.device(at, self.c), to

    def partner(self):
        return self.device(self.at, 1 - self.c)

    def group(self, by):
        j = rem(self.j + by, 8)
        return self.device((self.at[0], self.at[1], div(j, 2)), rem(j, 2)), j

    def barrier(self):
        sem = pltpu.get_barrier_semaphore()
        peers = [self.along(a, by)[0] for a in (X, Y) for by in STEPS] + [self.group(by)[0] for by in OTHERS]
        for d in peers:
            pl.semaphore_signal(sem, inc=1, device_id=d, device_id_type=MESH)
        pl.semaphore_wait(sem, len(peers))


class Job:
    def __init__(self, mat, order, rows, c0, c1):
        self.mat, self.order, self.rows, self.c0, self.c1 = mat, order, rows, c0, c1
        self.cols = c1 - c0
        self.axes = tuple(sorted(order))
        self.rings = 2

    def rest(self, p):
        return tuple(sorted(self.order[p + 1 :]))

    def block_shape(self, p):
        return (4,) * len(self.rest(p)) + (self.rows, self.cols)

    def unit_shape(self, p):
        rest = self.rest(p)
        if not rest:
            return (self.rows, self.cols // 2)
        return tuple(2 if a == self.order[-1] else 4 for a in rest) + (self.rows, self.cols)

    def unit(self, place, p, blk, h):
        co = {a: place.at[a] for a in self.order[:p]}
        co[self.order[p]] = blk
        for a in self.order[p + 1 :]:
            co[a] = pl.ds(0, 4)
        cols = (0, self.cols)
        if self.order[p + 1 :]:
            co[self.order[-1]] = pl.ds(2 * h, 2)
        elif h is not None:
            cols = (h * (self.cols // 2), (h + 1) * (self.cols // 2))
        return co, cols

    def whole(self, ref, unit, lead=()):
        co, (lo, hi) = unit
        return ref.at[(*lead, *(co[a] for a in self.axes), slice(None), pl.ds(self.c0 + lo, hi - lo))]

    def part(self, ref, p, side, unit):
        co, (lo, hi) = unit
        return ref.at[(side, *(co[a] for a in self.rest(p)), slice(None), pl.ds(lo, hi - lo))]


def jobs_of(shape_gate, shape_down):
    cols, down = shape_gate[-1], shape_down[-1]
    cut = (down // 128 + 1) // 2 * 128
    return (
        Job(0, (X, Y), shape_gate[-2], 0, cols),
        Job(1, (Y, X), shape_gate[-2], 0, cols),
        Job(2, (Z, X, Y), shape_down[-2], 0, cut),
        Job(2, (Z, Y, X), shape_down[-2], cut, down),
    )


def add_up(dst, srcs):
    *lead, rows, _ = dst.shape
    tiles = rows // 8
    count = tiles
    for d in lead:
        count *= d

    def body(i, _):
        at, up = [], div(i, tiles)
        for d in reversed(lead):
            at.append(rem(up, d))
            up = div(up, d)
        ix = (*reversed(at), pl.ds(pl.multiple_of(rem(i, tiles) * 8, 8), 8), slice(None))
        total = srcs[0][ix].astype(F32)
        for s in srcs[1:]:
            total = total + s[ix].astype(F32)
        dst[ix] = total.astype(dst.dtype)
        return 0

    lax.fori_loop(0, count, body, 0)


def reduce_kernel(jobs, g0, g1, g2, o0, o1, o2, osq, *s):
    s = list(s)
    take = lambda n: [s.pop(0) for _ in range(n)]
    hbm = (g0, g1, g2)
    mine, theirs = take(3), take(3)
    ra = [take(2) for _ in jobs]
    rb = [take(2) for _ in jobs]
    r3 = take(2)
    summed, pieces, got = take(3), take(2), take(2)
    piece_d, got_d = take(2)
    total, total_d, squares = take(3)
    load_sem, d2d_send, d2d_recv, ring_send, ring_recv, end_send, end_recv, third_send, third_recv, sq_send, sq_recv, down_send, down_recv = take(13)

    me = Place()
    me.barrier()
    c = me.c

    kinds = [(2, 0), (2, 1), (1, 1), (-1, 0), (1, 0), (-1, 1), (0, 0), (0, 1)]
    loads, swaps = {}, {}
    for k, (by, h) in enumerate(kinds):
        for n, job in enumerate(jobs):
            _, blk = me.along(job.order[0], by)
            unit = job.unit(me, 0, blk, h)
            swaps[n, k] = pltpu.make_async_remote_copy(
                job.whole(hbm[job.mat], unit, (1 - c,)), job.whole(theirs[job.mat], unit),
                d2d_send.at[n, k], d2d_recv.at[n, k], device_id=me.partner(), device_id_type=MESH)
            loads[n, k] = pltpu.make_async_copy(job.whole(hbm[job.mat], unit, (c,)), job.whole(mine[job.mat], unit), load_sem.at[n, k])
            swaps[n, k].start()
            loads[n, k].start()

    sent = []

    def terms(n, p, unit):
        job = jobs[n]
        refs = [job.whole(mine[job.mat], unit), job.whole(theirs[job.mat], unit)]
        for q in range(p):
            refs += [job.part(rb[n][q], q, side, unit) for side in (0, 1)]
        return refs

    def send(n, p, kind):
        job, way = jobs[n], kind % 2
        axis = job.order[p]
        to, _ = me.along(axis, 1 if way == RIGHT else -1)
        by, h = kinds[kind]
        _, blk = me.along(axis, by)
        unit = job.unit(me, p, blk, h)
        if p == 0:
            loads[n, kind].wait()
            swaps[n, kind].wait_recv()
        refs = terms(n, p, unit)
        if kind >= 4:
            ring[n, p, way].wait_recv()
            refs.append(ra[n][p].at[way])
        add_up(refs[0], refs)
        _, own = me.along(axis, 0)
        into = ra[n][p].at[way] if kind < 2 else job.part(rb[n][p], p, way, job.unit(me, p, own, h))
        ring[n, p, kind] = pltpu.make_async_remote_copy(
            refs[0], into, ring_send.at[n, p, kind], ring_recv.at[n, p, kind], device_id=to, device_id_type=MESH)
        ring[n, p, kind].start()
        sent.append(ring[n, p, kind])

    ring = {}
    for kind in range(6):
        for n in range(len(jobs)):
            send(n, 0, kind)
    for kind in (6, 7):
        for n in range(len(jobs)):
            loads[n, kind].wait()
            swaps[n, kind].wait_recv()
    for n in range(len(jobs)):
        for kind in range(2, 6):
            ring[n, 0, kind].wait_recv()
        for kind in range(4):
            send(n, 1, kind)
    for n in range(len(jobs)):
        for kind in (4, 5):
            send(n, 1, kind)

    for n in DOWN:
        job = jobs[n]
        for kind in range(2, 6):
            ring[n, 1, kind].wait_recv()
        for by in STEPS:
            to, blk = me.along(job.order[2], by)
            refs = terms(n, 2, job.unit(me, 2, blk, None))
            add_up(refs[0], refs)
            ring[n, 2, by] = pltpu.make_async_remote_copy(
                refs[0], r3[n - 2].at[by - 1], third_send.at[n - 2, by - 1], third_recv.at[n - 2, by - 1], device_id=to, device_id_type=MESH)
            ring[n, 2, by].start()
            sent.append(ring[n, 2, by])

    last = {}
    for n in PLAIN:
        job = jobs[n]
        for kind in range(2, 6):
            ring[n, 1, kind].wait_recv()
        unit = ({a: me.at[a] for a in job.axes}, (0, job.cols))
        refs = terms(n, 2, unit)
        add_up(summed[n].at[pl.ds(0, job.rows)], refs)
        summed[n][pl.ds(job.rows, 8), :] = jnp.zeros((8, job.cols), F32)
        for j in GROUP:
            pieces[n][j] = summed[n][7 * j : 7 * j + 8, :].astype(BF16)
        for by in OTHERS:
            to, j = me.group(by)
            last[n, by] = pltpu.make_async_remote_copy(
                pieces[n].at[j], got[n].at[me.j], end_send.at[n, by], end_recv.at[n, by], device_id=to, device_id_type=MESH)
            last[n, by].start()
            sent.append(last[n, by])
        got[n][me.j] = jnp.zeros(got[n].shape[1:], BF16)
        for j in GROUP:
            @pl.when(me.j == j)
            def _(j=j, n=n):
                total[n, c] = summed[n][7 * j : 7 * j + 8, :]
        total[n, 1 - c] = jnp.zeros(total.shape[2:], F32)

    rows = jobs[2].rows
    half = rows // 2
    for n in DOWN:
        job = jobs[n]
        for by in STEPS:
            ring[n, 2, by].wait_recv()
        unit = ({a: me.at[a] for a in job.axes}, (0, job.cols))
        refs = terms(n, 2, unit) + [r3[n - 2].at[k] for k in range(3)]
        add_up(summed[2].at[pl.ds(0, rows), pl.ds(job.c0, job.cols)], refs)
    summed[2][pl.ds(rows, 8), :] = jnp.zeros((8, summed[2].shape[1]), F32)
    pad = piece_d.shape[0]
    for k in range(2):
        @pl.when(c == k)
        def _(k=k):
            total_d[c] = summed[2][half * k : half * k + pad, :]
            piece_d[...] = summed[2][half * (1 - k) : half * (1 - k) + pad, :].astype(BF16)
    down = pltpu.make_async_remote_copy(piece_d, got_d, down_send, down_recv, device_id=me.partner(), device_id_type=MESH)
    down.start()
    sent.append(down)

    keep = lax.broadcasted_iota(jnp.int32, (8, 1), 0) < 7
    square = jnp.zeros((8, total.shape[-1]), F32)
    for n, out in ((0, o0), (1, o1)):
        for by in OTHERS:
            last[n, by].wait_recv()
        for layer in range(2):
            t = total[n, layer]
            for z in range(4):
                t = t + got[n][2 * z + layer].astype(F32)
            t = t.astype(BF16)
            out[layer] = t
            t = jnp.where(keep, t.astype(F32), 0.0)
            square = square + t * t
    square_d = jnp.zeros((8, total_d.shape[-1]), F32)
    down.wait_recv()
    total_d[1 - c] = got_d[...].astype(F32)
    for layer in range(2):
        for r in range(0, half, 8):
            t = total_d[layer, r : r + 8].astype(BF16)
            o2[layer, r : r + 8] = t
            t = t.astype(F32)
            if half - r < 8:
                t = jnp.where(lax.broadcasted_iota(jnp.int32, (8, 1), 0) < half - r, t, 0.0)
            square_d = square_d + t * t
    lanes = jnp.zeros((8, 128), F32)
    for k in range(0, square.shape[1], 128):
        lanes = lanes + square[:, k : k + 128]
    for k in range(0, square_d.shape[1], 128):
        lanes = lanes + square_d[:, k : k + 128]

    for step, (size, own) in enumerate(((4, me.at[0]), (4, me.at[1]), (8, me.j))):
        squares[step, own] = lanes
        copies = []
        for by in range(1, size):
            to = me.group(by)[0] if step == 2 else me.along(step, by)[0]
            copies.append(pltpu.make_async_remote_copy(
                squares.at[step, own], squares.at[step, own], sq_send.at[step, by], sq_recv.at[step, by], device_id=to, device_id_type=MESH))
            copies[-1].start()
        sent.extend(copies)
        for copy in copies:
            copy.wait_recv()
        lanes = squares[step, 0]
        for k in range(1, size):
            lanes = lanes + squares[step, k]
    osq[...] = lanes

    for copy in sent:
        copy.wait_send()
    for copy in swaps.values():
        copy.wait_send()


def gather_kernel(jobs, n0, n1, n2, o0, o1, o2, *s):
    s = list(s)
    take = lambda n: [s.pop(0) for _ in range(n)]
    outs = (o0, o1, o2)
    new = (n0, n1, n2)
    whole = take(3)
    pieces, piece_d, summed = take(2), *take(1), take(3)
    end_send, end_recv, down_send, down_recv, third_send, third_recv, ring_send, ring_recv, out_sem, d2d_send, d2d_recv = take(11)

    me = Place()
    me.barrier()
    c = me.c
    sent = []

    def go(copy):
        copy.start()
        sent.append(copy)
        return copy

    last = {}
    for n in PLAIN:
        for by in OTHERS:
            to, j = me.group(by)
            last[n, by] = go(pltpu.make_async_remote_copy(
                new[n].at[rem(j, 2)], pieces[n].at[me.j], end_send.at[n, by], end_recv.at[n, by], device_id=to, device_id_type=MESH))
        pieces[n][me.j] = new[n][c]
    down = go(pltpu.make_async_remote_copy(new[2].at[1 - c], piece_d.at[c], down_send, down_recv, device_id=me.partner(), device_id_type=MESH))
    piece_d[c] = new[2][c]

    rows = jobs[2].rows
    half, pad = rows // 2, piece_d.shape[1]
    down.wait_recv()
    for k in range(2):
        summed[2][half * k : half * k + pad, :] = piece_d[k].astype(F32)
    mat = whole[2].at[me.at]
    for r in range(0, rows, 8):
        mat[r : r + 8, :] = summed[2][r : r + 8, :].astype(BF16)
    third = {}
    for n in DOWN:
        job = jobs[n]
        ref = job.whole(whole[2], ({a: me.at[a] for a in job.axes}, (0, job.cols)))
        for by in STEPS:
            to, _ = me.along(job.order[2], by)
            third[n, by] = go(pltpu.make_async_remote_copy(ref, ref, third_send.at[n - 2, by], third_recv.at[n - 2, by], device_id=to, device_id_type=MESH))

    for n in PLAIN:
        job = jobs[n]
        for by in OTHERS:
            last[n, by].wait_recv()
        for j in GROUP:
            summed[n][7 * j : 7 * j + 8, :] = pieces[n][j].astype(F32)
        mat = whole[n].at[me.at[:2]]
        for r in range(0, job.rows, 8):
            mat[r : r + 8, :] = summed[n][r : r + 8, :].astype(BF16)

    ring = {}

    def send(n, p, kind):
        job, way = jobs[n], kind % 2
        to, _ = me.along(job.order[p], 1 if way == RIGHT else -1)
        by, h = ((0, 0), (0, 1), (0, 1), (0, 0), (-1, 0), (1, 1))[kind]
        _, blk = me.along(job.order[p], by)
        if kind >= 4:
            ring[n, p, way].wait_recv()
        ref = job.whole(whole[job.mat], job.unit(me, p, blk, h))
        ring[n, p, kind] = go(pltpu.make_async_remote_copy(
            ref, ref, ring_send.at[n, p, kind], ring_recv.at[n, p, kind], device_id=to, device_id_type=MESH))

    writes, swaps = [], []

    def put(n, k, by, h):
        job = jobs[n]
        _, blk = me.along(job.order[0], by)
        unit = job.unit(me, 0, blk, h)
        src, dst = job.whole(whole[job.mat], unit), job.whole(outs[job.mat], unit, (c,))
        swaps.append(go(pltpu.make_async_remote_copy(src, dst, d2d_send.at[n, k], d2d_recv.at[n, k], device_id=me.partner(), device_id_type=MESH)))
        writes.append(pltpu.make_async_copy(src, dst, out_sem.at[n, k]))
        writes[-1].start()

    order = (2, 3, 0, 1)
    for n in order:
        if n >= 2:
            for by in STEPS:
                third[n, by].wait_recv()
        for kind in range(4):
            send(n, 1, kind)
    for n in order:
        for kind in (4, 5):
            send(n, 1, kind)
    for n in order:
        for kind in range(2, 6):
            ring[n, 1, kind].wait_recv()
        for kind in range(4):
            send(n, 0, kind)
        for h in (0, 1):
            put(n, 6 + h, 0, h)
    came = ((-1, 0), (1, 1), (-1, 1), (1, 0), (2, 0), (2, 1))
    for kind in (4, 5):
        for n in order:
            send(n, 0, kind)
            put(n, kind - 4, *came[kind - 4])
    for kind in range(2, 6):
        for n in order:
            ring[n, 0, kind].wait_recv()
            put(n, kind, *came[kind])
    for copy in swaps:
        copy.wait_recv()
    for copy in writes:
        copy.wait()
    for copy in sent:
        copy.wait_send()


def adamw(w, m, v, g):
    m = 0.9 * m + 0.1 * g
    v = 0.95 * v + 0.05 * g * g
    step = m * lax.rsqrt(v + 1e-8) + 0.1 * w
    return (w - 0.02 * step).astype(BF16), m, v


def dma(*shape):
    return pltpu.SemaphoreType.DMA(shape) if shape else pltpu.SemaphoreType.DMA


def reduce_call(jobs, *g):
    cols, down, rows = g[0].shape[-1], g[2].shape[-1], jobs[2].rows
    pad = rows // 2 + 4
    mats = [pltpu.VMEM(x.shape[1:], BF16) for x in g]
    scratch = mats + mats
    for job in jobs:
        scratch += [pltpu.VMEM((2, *job.unit_shape(p)), BF16) for p in range(2)]
    for job in jobs:
        scratch += [pltpu.VMEM((2, *job.block_shape(p)), BF16) for p in range(2)]
    scratch += [pltpu.VMEM((3, rows, job.cols), BF16) for job in jobs[2:]]
    scratch += [pltpu.VMEM((jobs[0].rows + 8, cols), F32)] * 2 + [pltpu.VMEM((rows + 8, down), F32)]
    scratch += [pltpu.VMEM((8, 8, cols), BF16)] * 4
    scratch += [pltpu.VMEM((pad, down), BF16)] * 2
    scratch += [pltpu.VMEM((2, 2, 8, cols), F32), pltpu.VMEM((2, pad, down), F32), pltpu.VMEM((3, 8, 8, 128), F32)]
    n = len(jobs)
    scratch += [dma(n, 8)] * 3 + [dma(n, 2, 6)] * 2 + [dma(2, 8)] * 2 + [dma(2, 3)] * 2 + [dma(3, 8)] * 2 + [dma()] * 2
    return pl.pallas_call(
        functools.partial(reduce_kernel, jobs),
        out_shape=[jax.ShapeDtypeStruct((2, 8, cols), BF16)] * 2 + [jax.ShapeDtypeStruct((2, pad, down), BF16), jax.ShapeDtypeStruct((8, 128), F32)],
        in_specs=[pl.BlockSpec(memory_space=pl.ANY)] * 3,
        out_specs=[pl.BlockSpec(memory_space=pltpu.VMEM)] * 4,
        scratch_shapes=scratch,
        compiler_params=pltpu.CompilerParams(collective_id=0, has_side_effects=True, vmem_limit_bytes=VMEM_LIMIT),
        name="reduce",
    )(*g)


def gather_call(jobs, shapes, *new):
    cols, (pad, down), rows = new[0].shape[-1], new[2].shape[1:], jobs[2].rows
    scratch = [pltpu.VMEM(s, BF16) for s in shapes]
    scratch += [pltpu.VMEM((8, 8, cols), BF16)] * 2 + [pltpu.VMEM((2, pad, down), BF16)]
    scratch += [pltpu.VMEM((jobs[0].rows + 8, cols), F32)] * 2 + [pltpu.VMEM((rows + 8, down), F32)]
    n = len(jobs)
    scratch += [dma(2, 8)] * 2 + [dma()] * 2 + [dma(2, 4)] * 2 + [dma(n, 2, 6)] * 2 + [dma(n, 8)] * 3
    return pl.pallas_call(
        functools.partial(gather_kernel, jobs),
        out_shape=[jax.ShapeDtypeStruct((2, *s), BF16) for s in shapes],
        in_specs=[pl.BlockSpec(memory_space=pltpu.VMEM)] * 3,
        out_specs=[pl.BlockSpec(memory_space=pl.ANY)] * 3,
        scratch_shapes=scratch,
        compiler_params=pltpu.CompilerParams(collective_id=1, has_side_effects=True, vmem_limit_bytes=VMEM_LIMIT),
        name="gather",
    )(*new)


def solution(mesh):
    def step(*arrays):
        terms, weights, m, v = (arrays[i : i + 3] for i in (0, 3, 6, 9))
        full = [w.shape for w in weights]
        shapes = [(4, 4, full[0][1] // 16, full[0][2])] * 2 + [(4, 4, 4, full[2][1] // 64, full[2][2])]
        jobs = jobs_of(shapes[0], shapes[2])
        *sums, squares = reduce_call(jobs, *(t.reshape(2, *s) for t, s in zip(terms, shapes, strict=True)))
        factor = jnp.minimum(1.0, 0.5 * lax.rsqrt(jnp.sum(squares) / (128 * sum(one.size for one in m)) + 1e-30))
        me = lax.axis_index("dp")
        new = []
        for w, mm, vv, g in zip(weights, m, v, sums, strict=True):
            rows = mm.shape[1]
            own = lax.dynamic_slice_in_dim(w, me * rows, rows, 1).astype(F32)
            new.append(adamw(own, mm, vv, g[:, :rows].astype(F32) * factor))
        padded = [jnp.pad(one[0], ((0, 0), (0, g.shape[1] - one[0].shape[1]), (0, 0))) for one, g in zip(new, sums, strict=True)]
        whole = gather_call(jobs, shapes, *padded)
        whole = [w.reshape(s) for w, s in zip(whole, full, strict=True)]
        return (*whole, *(one[1] for one in new), *(one[2] for one in new))

    all_of, cut = P(None, None, None), P(None, "dp", None)
    return jax.shard_map(
        step,
        mesh=mesh,
        in_specs=(P(("rep", "dp"), None, None, None),) * 3 + (all_of,) * 3 + (cut,) * 6,
        out_specs=(P("rep", None, None),) * 3 + (P("rep", "dp", None),) * 6,
        check_vma=False,
    )
```

time: 635 us -> 204 us (0.32)
  waiting for transfers between devices: 422 us -> 0 us
  Pallas kernels: 0 us -> 168 us
  local copies, waits for them, and re-layouts: 121 us -> 30.2 us
  blocking collectives: 64.9 us -> 0 us
  between operations: 16.6 us -> 1.44 us
    unnamed x5 -> x0, waiting for transfers between devices: 236 us -> none
    all_gather x3 -> x0, waiting for transfers between devices: 186 us -> none  [step(): whole = [lax.all_gather(one[0], 'dp', axis=1, tiled=True) for one in new]]
    pallas_call x0 -> x2, Pallas kernels: none -> 168 us  [the longest x1 93.4 us: reduce_call(): pl.pallas_call(functools.partial(reduce_kernel, jobs), out_shape=[jax.Sha...]
    unnamed x26 -> x21, local copies, waits for them, and re-layouts: 119 us -> 28.3 us
    psum x1 -> x0, blocking collectives: 64.9 us -> none  [step(): squares = lax.psum(sum((jnp.sum(g * g) for g in gradients)), 'dp')]
  transfers between devices with their start and end apart: 4 -> 0, of which waited for: 4 -> 0; matrix products, arithmetic and copies ran while one was open for 4% -> 0% of each run, Pallas kernels for 0% -> 0%
where the time goes in v1:
time: 204 us
  Pallas kernels  168 us (82%)
  local copies, waits for them, and re-layouts  30.2 us (15%)
  other arithmetic  3.72 us (2%)
    pallas_call x1, Pallas kernels, reduce_call(): pl.pallas_call(functools.partial(reduce_kernel, jobs), out_shape=[jax.Sha...  93.4 us
    pallas_call x1, Pallas kernels, gather_call(): pl.pallas_call(functools.partial(gather_kernel, jobs), out_shape=[jax.Sha...  74.8 us
    unnamed x21, local copies, waits for them, and re-layouts  28.3 us

profile of v1, /device:TPU:1, one launch (start us, length us, event | category | flops | bytes accessed | tf_op | source)
XLA Modules:
  0.0 203.5 jit_solution(5007005844538739221)
XLA Ops:
  0.6 0.0 copy-start.4
  0.7 0.0 copy-start.5
  0.7 0.0 copy-start
  0.7 0.0 copy-start.1
  0.7 0.0 copy-start.2
  0.7 0.0 copy-start.3
  0.7 93.4 %reduce.1 = (bf16[2,8,2560]{2,1,0:T(8,128)(2,1)}, bf16[2,8,2560]{2,1,0:T(8,128)(2,1)}, bf16[2,24,896]{2,1,0:T(8,128)(2,1)}, f32[8,128]{1,0:T(8,128)}) custom-call(bf16[2,4,4,56,2560]{4,3,2,1,0:T(8,128)(2,1)} %bitcast.9, bf16[2,4,4,56,2560]{4,3,2,1,0:T(8,128)(2,1)} %bitcast.10, bf16[2,4,4,4,40,896]{5,4,3,2,1,0:T(8,128)(2,1)} %bitcast.11), custom_call_target="tpu_custom_call" | custom-call | tf_op jit(solution)/shard_map/reduce/pallas_call | solution.py:457
  94.1 1.3 reduce_sum.9
  96.1 0.0 copy-done.4
  96.1 0.0 copy-done.5
  96.1 1.1 fusion.2
  97.2 0.6 pad.13.n2
  97.8 0.7 copy.32
  98.6 0.7 copy.29
  99.3 0.0 copy-done
  99.3 0.0 copy-done.1
  99.3 0.0 copy-done.2
  99.3 0.0 copy-done.3
  99.3 1.4 fusion.7
  100.7 0.7 pad.11.n0
  101.3 0.7 pad.12.n1
  102.0 0.8 copy.30
  102.7 0.8 copy.27
  103.5 0.8 copy.31
  104.3 0.8 copy.28
  105.1 74.8 %gather.1 = (bf16[2,4,4,56,2560]{4,3,2,1,0:T(8,128)(2,1)}, bf16[2,4,4,56,2560]{4,3,2,1,0:T(8,128)(2,1)}, bf16[2,4,4,4,40,896]{5,4,3,2,1,0:T(8,128)(2,1)}) custom-call(bf16[2,8,2560]{2,1,0:T(8,128)(2,1)} %pad.11.n0, bf16[2,8,2560]{2,1,0:T(8,128)(2,1)} %pad.12.n1, bf16[2,24,896]{2,1,0:T(8,128)(2,1)} %pad.13.n2), custom_call_target="tpu_custom_call" | custom-call | tf_op jit(solution)/shard_map/gather/pallas_call | solution.py:475
  179.8 7.9 %copy.60 = bf16[2,896,2560]{2,1,0:T(8,128)(2,1)} copy(bf16[2,896,2560]{2,1,0:T(8,128)(2,1)} %bitcast.8) | data formatting | bytes 18350080
  187.7 7.8 %copy.61 = bf16[2,896,2560]{2,1,0:T(8,128)(2,1)} copy(bf16[2,896,2560]{2,1,0:T(8,128)(2,1)} %bitcast.7) | data formatting | bytes 18350080
  195.5 8.0 %copy.62 = bf16[2,2560,896]{2,1,0:T(8,128)(2,1)} copy(bf16[2,2560,896]{2,1,0:T(8,128)(2,1)} %bitcast.6) | data formatting | bytes 18350080
Async XLA Ops:
  0.6 95.4 %copy-start.4 = (f32[2,20,896]{2,0,1:T(2,128)S(1)}, f32[2,20,896]{2,0,1:T(2,128)}, u32[]{:S(2)}) copy-start(f32[2,20,896]{2,0,1:T(2,128)} %param.23) | copy-start | bytes 430084
  0.7 95.4 %copy-start.5 = (f32[2,20,896]{2,0,1:T(2,128)S(1)}, f32[2,20,896]{2,0,1:T(2,128)}, u32[]{:S(2)}) copy-start(f32[2,20,896]{2,0,1:T(2,128)} %param.20) | copy-start | bytes 430084
  0.7 98.6 %copy-start = (f32[2,7,2560]{2,0,1:T(2,128)S(1)}, f32[2,7,2560]{2,0,1:T(2,128)}, u32[]{:S(2)}) copy-start(f32[2,7,2560]{2,0,1:T(2,128)} %param.21) | copy-start | bytes 430084
  0.7 98.6 %copy-start.1 = (f32[2,7,2560]{2,0,1:T(2,128)S(1)}, f32[2,7,2560]{2,0,1:T(2,128)}, u32[]{:S(2)}) copy-start(f32[2,7,2560]{2,0,1:T(2,128)} %param.18) | copy-start | bytes 430084
  0.7 98.6 %copy-start.2 = (f32[2,7,2560]{2,0,1:T(2,128)S(1)}, f32[2,7,2560]{2,0,1:T(2,128)}, u32[]{:S(2)}) copy-start(f32[2,7,2560]{2,0,1:T(2,128)} %param.22) | copy-start | bytes 430084
  0.7 98.6 %copy-start.3 = (f32[2,7,2560]{2,0,1:T(2,128)S(1)}, f32[2,7,2560]{2,0,1:T(2,128)}, u32[]{:S(2)}) copy-start(f32[2,7,2560]{2,0,1:T(2,128)} %param.19) | copy-start | bytes 430084
